TPU v7x, 32 devices: a whole 2x2x4 slice. The times are simulated.
32 devices in a mesh: kx: 8 (over z, x), cz: 4 (over y, core).
Axes of the slice: x: 2, y: 2, z: 4, core: 2. Of those that a mesh axis runs over, the one named last changes fastest.
Arguments:
- field_modes: bfloat16 [512, 4, 12288], P('cz', None, 'kx'), may hold values from -6 to 6
- cotangent: bfloat16 [512, 4, 12288], P('cz', None, 'kx'), may hold values from -6 to 6
Outputs:
- mode_gradient: bfloat16 [512, 4, 12288], P('cz', None, 'kx')
All inputs are finite; a program needn't handle non-finite values.
Results may differ from a plain program's by a relative error of at most 0.009.
Values may be sent and summed in bfloat16 or wider, within the bound.
A program may use at most 128 MiB of HBM per device.

v0:
```python
import math
import jax
import jax.numpy as jnp
from jax import lax
from jax.sharding import PartitionSpec as P

NZ = 512
MZ = 768
NX = 768
Y = 16


def cosine_table():
    row_index = jnp.arange(MZ, dtype=jnp.int32)
    col_index = jnp.arange(NZ, dtype=jnp.int32)
    position = col_index[None, :] * (2 * row_index[:, None] + 1) % (4 * MZ)
    return jnp.cos(jnp.pi * position.astype(jnp.float32) / (2 * MZ))


def hartley_table():
    points = jnp.arange(NX, dtype=jnp.int32)
    position = points[:, None] * points[None, :] % NX
    phases = 2.0 * jnp.pi * position.astype(jnp.float32) / NX
    return ((jnp.cos(phases) + jnp.sin(phases)) / math.sqrt(NX)).astype(jnp.bfloat16)


def product_gradient(fields, adjoint):
    vertical = fields[2]
    return jnp.stack(
        [
            adjoint[0] * vertical,
            adjoint[1] * vertical,
            adjoint[0] * fields[0]
            + adjoint[1] * fields[1]
            + 2.0 * adjoint[2] * vertical
            + adjoint[3] * fields[3],
            adjoint[3] * vertical,
        ]
    ).astype(jnp.bfloat16)


def on_device(field_modes, cotangent):
    local_modes = field_modes.shape[0]
    field_count = field_modes.shape[1]
    local_columns = field_modes.shape[2] // Y
    field_grid = field_modes.reshape(local_modes, field_count, local_columns, Y)
    cotangent_grid = cotangent.reshape(local_modes, field_count, local_columns, Y)
    cosines = cosine_table()
    synthesis = (cosines * math.sqrt(2.0 / NZ)).astype(jnp.bfloat16)
    projection = (cosines * math.sqrt(2.0 / MZ)).astype(jnp.bfloat16)
    hartley = hartley_table()
    lifted = jnp.concatenate(
        [
            jnp.einsum(
                "zk,kfxy->yfxz",
                synthesis,
                lax.all_to_all(field_grid, "cz", split_axis=3, concat_axis=0, tiled=True),
                preferred_element_type=jnp.float32,
            ).astype(jnp.bfloat16),
            jnp.einsum(
                "zk,kfxy->yfxz",
                projection,
                lax.all_to_all(cotangent_grid, "cz", split_axis=3, concat_axis=0, tiled=True),
                preferred_element_type=jnp.float32,
            ).astype(jnp.bfloat16),
        ],
        axis=1,
    )
    piece = lax.all_to_all(lifted, "kx", split_axis=3, concat_axis=2, tiled=True)
    fields = jnp.einsum(
        "xm,yfmz->fyzx", hartley, piece[:, :field_count], preferred_element_type=jnp.float32
    )
    adjoint = jnp.einsum(
        "xm,yfmz->fyzx", hartley, piece[:, field_count:], preferred_element_type=jnp.float32
    )
    gradient = product_gradient(fields, adjoint)
    turned = jnp.einsum(
        "xm,fyzx->yfmz", hartley, gradient, preferred_element_type=jnp.float32
    ).astype(jnp.bfloat16)
    returned = lax.all_to_all(turned, "kx", split_axis=2, concat_axis=3, tiled=True)
    spectral = jnp.einsum(
        "zk,yfxz->kfxy", synthesis, returned, preferred_element_type=jnp.float32
    ).astype(jnp.bfloat16)
    result = lax.all_to_all(spectral, "cz", split_axis=0, concat_axis=3, tiled=True)
    return result.reshape(local_modes, field_count, local_columns * Y)


def solution(mesh):
    return jax.shard_map(
        on_device,
        mesh=mesh,
        in_specs=(P("cz", None, "kx"), P("cz", None, "kx")),
        out_specs=P("cz", None, "kx"),
        check_vma=False,
    )
```

profile of v0, /device:TPU:0, one launch (start us, length us, event | category | flops | bytes accessed | tf_op | source)
XLA Modules:
  0.0 435.8 jit_solution(16268019331299790281)
XLA Ops:
  0.0 3.0 copy.18
  3.0 1.6 copy.19
  4.5 4.3 all-to-all-start
  8.8 3.0 copy.22
  11.7 1.6 copy.23
  13.3 15.5 %all-to-all-done = bf16[128,4,96,16]{0,2,1,3:T(8,128)(2,1)S(1)} async-done(((bf16[128,4,96,16]{0,2,1,3:T(8,128)(2,1)}), bf16[128,4,96,16]{0,2,1,3:T(8,128)(2,1)S(1)}, u32[]{:S(2)}, u32[]{:S(2)}) %all-to-all-start) | async-done | bytes 1572896 | tf_op jit(solution)/shard_map/all_to_all | solution.py:57
  28.8 3.6 all-to-all-start.1
  32.4 2.4 copy.21
  34.8 3.6 all_to_all.66
  38.4 14.0 %all-to-all-done.1 = bf16[128,4,96,16]{0,2,1,3:T(8,128)(2,1)S(1)} async-done(((bf16[128,4,96,16]{0,2,1,3:T(8,128)(2,1)}), bf16[128,4,96,16]{0,2,1,3:T(8,128)(2,1)S(1)}, u32[]{:S(2)}, u32[]{:S(2)}) %all-to-all-start.1) | async-done | bytes 1572896 | tf_op jit(solution)/shard_map/all_to_all | solution.py:63
  52.4 1.2 copy.25
  53.6 0.0 copy-start.1
  53.6 2.0 all_to_all.70
  55.6 0.0 copy-done.1
  55.6 0.0 copy-start.2
  55.6 9.7 %convert_bitcast_fusion.2 = bf16[4,4,96,768]{3,2,0,1:T(8,128)(2,1)S(1)} fusion(bf16[512,4,96,4]{0,2,3,1:T(8,128)(2,1)S(1)} %copy-done.1, s32[768]{0:T(1024)S(1)} %multiply_add_fusion), kind=kOutput, calls=%fused_computation.16 | convolution fusion | flops 1213464576 | bytes 3935232 | tf_op jit(solution)/shard_map/zk,kfxy->yfxz/dot_general | solution.py:54
  65.4 0.0 copy-done.2
  65.4 9.7 %convert_bitcast_fusion.1 = bf16[4,4,96,768]{3,2,0,1:T(8,128)(2,1)S(1)} fusion(bf16[512,4,96,4]{0,2,3,1:T(8,128)(2,1)S(1)} %copy-done.2, s32[768]{0:T(1024)S(1)} %multiply_add_fusion), kind=kOutput, calls=%fused_computation.15 | convolution fusion | flops 1213464576 | bytes 3935232 | tf_op jit(solution)/shard_map/zk,kfxy->yfxz/dot_general | solution.py:60
  75.1 2.6 pad_maximum_fusion
  77.7 10.9 %copy.26 = bf16[4,8,96,768]{2,0,1,3:T(4,128)(2,1)} copy(bf16[4,8,96,768]{3,2,0,1:T(8,128)(2,1)} %pad_maximum_fusion) | data formatting | bytes 9437184 | tf_op jit(solution)/shard_map/concatenate | solution.py:52
  88.7 144.9 %all_to_all.87 = bf16[4,8,96,768]{2,0,1,3:T(4,128)(2,1)S(1)} all-to-all(bf16[4,8,96,768]{2,0,1,3:T(4,128)(2,1)} %copy.26), channel_id=1, replica_groups=mesh['kx'=8,'cz'=4] {'kx'}, dimensions={3} | all-to-all | bytes 9437184 | tf_op jit(solution)/shard_map/all_to_all | solution.py:69
  233.6 6.7 %copy.45 = bf16[4,8,96,8,96]{2,3,4,1,0:T(8,128)(2,1)} copy(bf16[4,8,96,8,96]{2,0,1,4,3:T(4,128)(2,1)S(1)} %bitcast.65) | data formatting | bytes 9437184 | tf_op jit(solution)/shard_map/all_to_all | solution.py:69
  240.3 10.8 %all_to_all.74 = bf16[4,8,768,96]{2,3,1,0:T(8,128)(2,1)} reshape(bf16[4,8,8,96,96]{3,2,4,1,0:T(8,128)(2,1)} %bitcast.66) | data formatting | bytes 9437184 | tf_op jit(solution)/shard_map/all_to_all | solution.py:69
  251.1 0.0 copy-start
  251.1 12.7 %convolution_bitcast_fusion = f32[4,4,96,768]{3,2,0,1:T(8,128)S(1)} fusion(bf16[4,8,768,96]{2,3,1,0:T(8,128)(2,1)} %all_to_all.74), kind=kOutput, calls=%fused_computation.18 | convolution fusion | flops 1819017216 | bytes 9437184 | tf_op jit(solution)/shard_map/xm,yfmz->fyzx/dot_general | solution.py:70
  263.8 0.0 copy-done
  263.8 25.5 %convolution_bitcast_fusion.1 = f32[4,4,96,768]{3,2,0,1:T(8,128)S(1)} fusion(bf16[4,8,768,96]{2,3,1,0:T(8,128)(2,1)S(1)} %copy-done), kind=kOutput, calls=%fused_computation.19 | convolution fusion | flops 1819017216 | bytes 9437184 | tf_op jit(solution)/shard_map/xm,yfmz->fyzx/dot_general | solution.py:73
  289.3 0.9 multiply_convert_fusion.5
  290.2 12.3 %convert_bitcast_fusion = bf16[4,4,768,96]{2,3,0,1:T(8,128)(2,1)} fusion(bf16[1,4,96,768]{3,2,0,1:T(8,128)(2,1)S(1)} %get-tuple-element.6, bf16[1,4,96,768]{3,2,0,1:T(8,128)(2,1)S(1)} %get-tuple-element.7, bf16[1,4,96,768]{3,2,0,1:T(8,128)(2,1)S(1)} %get-tuple-element.8, bf16[1,4,96,768]{3,2,0,1:T(8,128)(2,1)S(1)} %get-tuple-element.5), kind=kOutput, calls=%fused_computation.10 | convolution fusion | flops 1823735808 | bytes 4718592 | tf_op jit(solution)/shard_map/xm,fyzx->yfmz/dot_general | solution.py:77
  302.5 5.0 %copy.29 = bf16[4,4,768,96]{3,0,1,2:T(4,128)(2,1)S(1)} copy(bf16[4,4,768,96]{2,3,0,1:T(8,128)(2,1)} %convert_bitcast_fusion) | data formatting | bytes 4718592 | tf_op jit(solution)/shard_map/convert_element_type | solution.py:79
  307.5 73.6 %all_to_all.88 = bf16[4,4,768,96]{3,0,1,2:T(4,128)(2,1)S(1)} all-to-all(bf16[4,4,768,96]{3,0,1,2:T(4,128)(2,1)S(1)} %copy.29), channel_id=1, replica_groups=mesh['kx'=8,'cz'=4] {'kx'}, dimensions={2} | all-to-all | bytes 4718592 | tf_op jit(solution)/shard_map/all_to_all | solution.py:80
  381.1 2.0 copy.46
  383.1 3.6 all_to_all.78
  386.7 9.9 %fusion.15 = bf16[512,4,96,4]{0,2,1,3:T(8,128)(2,1)} fusion(bf16[4,4,96,768]{3,2,1,0:T(8,128)(2,1)} %all_to_all.78, s32[768]{0:T(1024)S(1)} %multiply_add_fusion), kind=kOutput, calls=%fused_computation.30 | convolution fusion | flops 1213071360 | bytes 3935232 | tf_op jit(solution)/shard_map/zk,yfxz->kfxy/dot_general | solution.py:81
  396.6 3.3 copy.31
  400.0 28.9 %all_to_all.89 = bf16[512,4,96,4]{2,1,3,0:T(4,128)(2,1)} all-to-all(bf16[512,4,96,4]{2,1,3,0:T(4,128)(2,1)S(1)} %copy.31), channel_id=1, replica_groups=mesh['kx'=8,'cz'=4] {'cz'}, dimensions={0} | all-to-all | bytes 3145728 | tf_op jit(solution)/shard_map/all_to_all | solution.py:84
  428.9 4.0 copy.32
  432.9 2.5 copy.33
  (1 shorter events, 0.0 us)
Async XLA Ops:
  4.5 24.3 %all-to-all-start = ((bf16[128,4,96,16]{0,2,1,3:T(8,128)(2,1)}), bf16[128,4,96,16]{0,2,1,3:T(8,128)(2,1)S(1)}, u32[]{:S(2)}, u32[]{:S(2)}) async-start(bf16[128,4,96,16]{0,2,1,3:T(8,128)(2,1)} %copy.19), calls=%async_computation | async-start | bytes 3145728 | tf_op jit(solution)/shard_map/all_to_all | solution.py:57
  28.8 23.6 %all-to-all-start.1 = ((bf16[128,4,96,16]{0,2,1,3:T(8,128)(2,1)}), bf16[128,4,96,16]{0,2,1,3:T(8,128)(2,1)S(1)}, u32[]{:S(2)}, u32[]{:S(2)}) async-start(bf16[128,4,96,16]{0,2,1,3:T(8,128)(2,1)} %copy.23), calls=%async_computation.1 | async-start | bytes 3145728 | tf_op jit(solution)/shard_map/all_to_all | solution.py:63
  53.6 2.0 copy-start.1
  55.6 9.7 %copy-start.2 = (bf16[512,4,96,4]{0,2,3,1:T(8,128)(2,1)S(1)}, bf16[512,4,96,4]{0,2,3,1:T(8,128)(2,1)}, u32[]{:S(2)}) copy-start(bf16[512,4,96,4]{0,2,3,1:T(8,128)(2,1)} %all_to_all.70) | copy-start | bytes 4718596
  251.1 12.7 %copy-start = (bf16[4,8,768,96]{2,3,1,0:T(8,128)(2,1)S(1)}, bf16[4,8,768,96]{2,3,1,0:T(8,128)(2,1)}, u32[]{:S(2)}) copy-start(bf16[4,8,768,96]{2,3,1,0:T(8,128)(2,1)} %all_to_all.74) | copy-start | bytes 14155780
where the time goes:
time: 444 us; the launch traced here: 436 us
  blocking collectives  247 us (56%)
  matrix products  79.8 us (18%)
  local copies, waits for them, and re-layouts  67.2 us (15%)
  waiting for transfers between devices  29.5 us (7%)
  starting transfers between devices  7.83 us (2%)
    all_to_all x1, blocking collectives, on_device(): lax.all_to_all(lifted, 'kx', split_axis=3, concat_axis=2, tiled=True)  145 us
    all_to_all x1, blocking collectives, on_device(): lax.all_to_all(turned, 'kx', split_axis=2, concat_axis=3, tiled=True)  73.6 us
    all_to_all x1, blocking collectives, on_device(): lax.all_to_all(spectral, 'cz', split_axis=0, concat_axis=3, tiled=True)  28.9 us
    dot_general x1, matrix products, on_device(): jnp.einsum('xm,yfmz->fyzx', hartley, piece[:, field_count:], preferred_el...  25.5 us
    all_to_all x2, local copies, waits for them, and re-layouts, on_device(): lax.all_to_all(lifted, 'kx', split_axis=3, concat_axis=2, tiled=True)  17.5 us
    all_to_all x1, waiting for transfers between devices, on_device(): lax.all_to_all(field_grid, 'cz', split_axis=3, concat_axis=0, tiled=True)  15.5 us
    all_to_all x1, waiting for transfers between devices, on_device(): lax.all_to_all(cotangent_grid, 'cz', split_axis=3, concat_axis=0, tiled=T...  14 us
    dot_general x1, matrix products, on_device(): jnp.einsum('xm,yfmz->fyzx', hartley, piece[:, :field_count], preferred_el...  12.7 us
  transfers between devices with their start and end apart: 2, of which 2 were waited for; matrix products, arithmetic and copies ran while one was open for 2% of the time, Pallas kernels for 0%

commit v1 on v0

--- a/solution.py
+++ b/solution.py
@@ -8,6 +8,30 @@
 MZ = 768
 NX = 768
 Y = 16
+
+
+def split_up(x, dim, devices):
+    lengths = x.shape
+    tiles = x.reshape(*lengths[:dim], devices, lengths[dim] // devices, *lengths[dim + 1 :])
+    return jnp.moveaxis(tiles, dim, 0)
+
+
+def laid_out(blocks, dim):
+    blocks = jnp.moveaxis(blocks, 0, dim)
+    shape = blocks.shape
+    return blocks.reshape(*shape[:dim], shape[dim] * shape[dim + 1], *shape[dim + 2 :])
+
+
+def exchange_directly(x, axis, split_dim, concat_dim):
+    size, index = (lax.axis_size(axis), lax.axis_index(axis))
+    blocks = split_up(x, split_dim, size)
+    out = blocks
+    for hop in range(1, size):
+        target, source = ((index + hop) % size, (index - hop) % size)
+        sent = lax.dynamic_index_in_dim(blocks, target, 0)
+        partner_block = lax.ppermute(sent, axis, [(i, (i + hop) % size) for i in range(size)])
+        out = lax.dynamic_update_slice_in_dim(out, partner_block, source, axis=0)
+    return laid_out(out, concat_dim)
 
 
 def cosine_table():
@@ -81,7 +105,7 @@
     spectral = jnp.einsum(
         "zk,yfxz->kfxy", synthesis, returned, preferred_element_type=jnp.float32
     ).astype(jnp.bfloat16)
-    result = lax.all_to_all(spectral, "cz", split_axis=0, concat_axis=3, tiled=True)
+    result = exchange_directly(spectral, "cz", 0, 3)
     return result.reshape(local_modes, field_count, local_columns * Y)
 
 

time: 444 us -> 432 us (0.973)
  the two profiles are of different devices: /device:TPU:0 before, /device:TPU:1 now
where the time goes in v1:
time: 432 us; the launch traced here: 424 us
  blocking collectives  144 us (33%)
  waiting for transfers between devices  113 us (26%)
  matrix products  76.8 us (18%)
  local copies, waits for them, and re-layouts  69.3 us (16%)
  starting transfers between devices  16.7 us (4%)
    all_to_all x1, blocking collectives, on_device(): lax.all_to_all(lifted, 'kx', split_axis=3, concat_axis=2, tiled=True)  144 us
    all_to_all x1, waiting for transfers between devices, on_device(): lax.all_to_all(turned, 'kx', split_axis=2, concat_axis=3, tiled=True)  69.2 us
    dot_general x1, matrix products, on_device(): jnp.einsum('xm,yfmz->fyzx', hartley, piece[:, :field_count], preferred_el...  25.5 us
    all_to_all x2, local copies, waits for them, and re-layouts, on_device(): lax.all_to_all(lifted, 'kx', split_axis=3, concat_axis=2, tiled=True)  17.5 us
    ppermute x3, waiting for transfers between devices, exchange_directly(): lax.ppermute(sent, axis, [(i, (i + hop) % size) for i in range(size)])  16.3 us
    all_to_all x1, waiting for transfers between devices, on_device(): lax.all_to_all(cotangent_grid, 'cz', split_axis=3, concat_axis=0, tiled=T...  14.3 us
    all_to_all x1, waiting for transfers between devices, on_device(): lax.all_to_all(field_grid, 'cz', split_axis=3, concat_axis=0, tiled=True)  13.1 us
    dot_general x1, matrix products, on_device(): jnp.einsum('xm,yfmz->fyzx', hartley, piece[:, field_count:], preferred_el...  12.7 us
  transfers between devices with their start and end apart: 6, of which 6 were waited for; matrix products, arithmetic and copies ran while one was open for 2% of the time, Pallas kernels for 0%

profile of v1, /device:TPU:1, one launch (start us, length us, event | category | flops | bytes accessed | tf_op | source)
XLA Modules:
  0.0 423.8 jit_solution(9882286519032256627)
XLA Ops:
  0.0 3.0 copy.25
  3.0 1.6 copy.26
  4.5 4.3 %all-to-all-start.1 = ((bf16[128,4,96,16]{0,2,1,3:T(8,128)(2,1)}), bf16[128,4,96,16]{0,2,1,3:T(8,128)(2,1)S(1)}, u32[]{:S(2)}, u32[]{:S(2)}) async-start(bf16[128,4,96,16]{0,2,1,3:T(8,128)(2,1)} %copy.26), calls=%async_computation.1 | async-start | bytes 3145728 | tf_op jit(solution)/shard_map/all_to_all | solution.py:87
  8.8 3.0 copy.21
  11.8 1.6 copy.22
  13.3 14.3 %all-to-all-done.1 = bf16[128,4,96,16]{0,2,1,3:T(8,128)(2,1)S(1)} async-done(((bf16[128,4,96,16]{0,2,1,3:T(8,128)(2,1)}), bf16[128,4,96,16]{0,2,1,3:T(8,128)(2,1)S(1)}, u32[]{:S(2)}, u32[]{:S(2)}) %all-to-all-start.1) | async-done | bytes 1572896 | tf_op jit(solution)/shard_map/all_to_all | solution.py:87
  27.6 4.8 %all-to-all-start = ((bf16[128,4,96,16]{0,2,1,3:T(8,128)(2,1)}), bf16[128,4,96,16]{0,2,1,3:T(8,128)(2,1)S(1)}, u32[]{:S(2)}, u32[]{:S(2)}) async-start(bf16[128,4,96,16]{0,2,1,3:T(8,128)(2,1)} %copy.22), calls=%async_computation | async-start | bytes 3145728 | tf_op jit(solution)/shard_map/all_to_all | solution.py:81
  32.4 2.4 copy.28
  34.7 3.7 all_to_all.59
  38.4 13.1 %all-to-all-done = bf16[128,4,96,16]{0,2,1,3:T(8,128)(2,1)S(1)} async-done(((bf16[128,4,96,16]{0,2,1,3:T(8,128)(2,1)}), bf16[128,4,96,16]{0,2,1,3:T(8,128)(2,1)S(1)}, u32[]{:S(2)}, u32[]{:S(2)}) %all-to-all-start) | async-done | bytes 1572896 | tf_op jit(solution)/shard_map/all_to_all | solution.py:81
  51.5 1.2 copy.24
  52.7 0.0 copy-start.1
  52.7 2.0 all_to_all.55
  54.7 0.0 copy-done.1
  54.7 0.0 copy-start.2
  54.7 9.7 %convert_bitcast_fusion.1 = bf16[4,4,96,768]{3,2,0,1:T(8,128)(2,1)S(1)} fusion(bf16[512,4,96,4]{0,2,3,1:T(8,128)(2,1)S(1)} %copy-done.1, s32[768]{0:T(1024)S(1)} %multiply_add_fusion), kind=kOutput, calls=%fused_computation.15 | convolution fusion | flops 1213464576 | bytes 3935232 | tf_op jit(solution)/shard_map/zk,kfxy->yfxz/dot_general | solution.py:84
  64.4 0.0 copy-done.2
  64.4 9.7 %convert_bitcast_fusion.2 = bf16[4,4,96,768]{3,2,0,1:T(8,128)(2,1)S(1)} fusion(bf16[512,4,96,4]{0,2,3,1:T(8,128)(2,1)S(1)} %copy-done.2, s32[768]{0:T(1024)S(1)} %multiply_add_fusion), kind=kOutput, calls=%fused_computation.16 | convolution fusion | flops 1213464576 | bytes 3935232 | tf_op jit(solution)/shard_map/zk,kfxy->yfxz/dot_general | solution.py:78
  74.1 2.6 pad_maximum_fusion
  76.8 10.9 %copy.29 = bf16[4,8,96,768]{2,0,1,3:T(4,128)(2,1)} copy(bf16[4,8,96,768]{3,2,0,1:T(8,128)(2,1)} %pad_maximum_fusion) | data formatting | bytes 9437184 | tf_op jit(solution)/shard_map/concatenate | solution.py:76
  87.7 144.0 %all_to_all.72 = bf16[4,8,96,768]{2,0,1,3:T(4,128)(2,1)S(1)} all-to-all(bf16[4,8,96,768]{2,0,1,3:T(4,128)(2,1)} %copy.29), channel_id=1, replica_groups=mesh['kx'=8,'cz'=4] {'kx'}, dimensions={3} | all-to-all | bytes 9437184 | tf_op jit(solution)/shard_map/all_to_all | solution.py:93
  231.7 6.7 %copy.50 = bf16[4,8,96,8,96]{2,3,4,1,0:T(8,128)(2,1)} copy(bf16[4,8,96,8,96]{2,0,1,4,3:T(4,128)(2,1)S(1)} %bitcast.68) | data formatting | bytes 9437184 | tf_op jit(solution)/shard_map/all_to_all | solution.py:93
  238.4 10.8 %all_to_all.63 = bf16[4,8,768,96]{2,3,1,0:T(8,128)(2,1)} reshape(bf16[4,8,8,96,96]{3,2,4,1,0:T(8,128)(2,1)} %bitcast.69) | data formatting | bytes 9437184 | tf_op jit(solution)/shard_map/all_to_all | solution.py:93
  249.3 0.0 copy-start
  249.3 12.7 %convolution_bitcast_fusion.1 = f32[4,4,96,768]{3,2,0,1:T(8,128)S(1)} fusion(bf16[4,8,768,96]{2,3,1,0:T(8,128)(2,1)} %all_to_all.63), kind=kOutput, calls=%fused_computation.19 | convolution fusion | flops 1819017216 | bytes 9437184 | tf_op jit(solution)/shard_map/xm,yfmz->fyzx/dot_general | solution.py:97
  262.0 0.0 copy-done
  262.0 25.5 %convolution_bitcast_fusion = f32[4,4,96,768]{3,2,0,1:T(8,128)S(1)} fusion(bf16[4,8,768,96]{2,3,1,0:T(8,128)(2,1)S(1)} %copy-done), kind=kOutput, calls=%fused_computation.18 | convolution fusion | flops 1819017216 | bytes 9437184 | tf_op jit(solution)/shard_map/xm,yfmz->fyzx/dot_general | solution.py:94
  287.5 0.9 multiply_convert_fusion.5
  288.3 10.9 %convert_bitcast_fusion = bf16[4,4,768,96]{2,3,0,1:T(8,128)(2,1)S(1)} fusion(bf16[1,4,96,768]{3,2,0,1:T(8,128)(2,1)S(1)} %get-tuple-element.6, bf16[1,4,96,768]{3,2,0,1:T(8,128)(2,1)S(1)} %get-tuple-element.7, bf16[1,4,96,768]{3,2,0,1:T(8,128)(2,1)S(1)} %get-tuple-element.8, bf16[1,4,96,768]{3,2,0,1:T(8,128)(2,1)S(1)} %get-tuple-element.5), kind=kOutput, calls=%fused_computation.10 | convolution fusion | flops 1823735808 | bytes 4718592 | tf_op jit(solution)/shard_map/xm,fyzx->yfmz/dot_general | solution.py:101
  299.3 4.5 %copy.32 = bf16[4,4,768,96]{3,0,1,2:T(4,128)(2,1)} copy(bf16[4,4,768,96]{2,3,0,1:T(8,128)(2,1)S(1)} %convert_bitcast_fusion) | data formatting | bytes 4718592 | tf_op jit(solution)/shard_map/convert_element_type | solution.py:103
  303.8 3.8 all-to-all-start.3
  307.6 69.2 %all-to-all-done.3 = bf16[4,4,768,96]{3,0,1,2:T(4,128)(2,1)S(1)} async-done(((bf16[4,4,768,96]{3,0,1,2:T(4,128)(2,1)}), bf16[4,4,768,96]{3,0,1,2:T(4,128)(2,1)S(1)}, u32[]{:S(2)}, u32[]{:S(2)}) %all-to-all-start.3) | async-done | bytes 2359328 | tf_op jit(solution)/shard_map/all_to_all | solution.py:104
  376.9 3.7 copy.51
  380.5 5.0 %all_to_all.67 = bf16[4,4,96,768]{3,2,1,0:T(8,128)(2,1)S(1)} reshape(bf16[4,4,96,8,96]{4,3,2,1,0:T(8,128)(2,1)} %bitcast.71) | data formatting | bytes 4718592 | tf_op jit(solution)/shard_map/all_to_all | solution.py:104
  385.5 8.3 %fusion.15 = bf16[512,4,96,4]{0,2,1,3:T(8,128)(2,1)} fusion(bf16[4,4,96,768]{3,2,1,0:T(8,128)(2,1)S(1)} %all_to_all.67, s32[768]{0:T(1024)S(1)} %multiply_add_fusion), kind=kOutput, calls=%fused_computation.30 | convolution fusion | flops 1213071360 | bytes 3935232 | tf_op jit(solution)/shard_map/zk,yfxz->kfxy/dot_general | solution.py:105
  393.8 2.6 reshape.18
  396.4 2.0 copy.35
  398.4 0.5 constant_dynamic-slice_fusion
  399.0 2.9 collective-permute-start
  401.8 0.9 collective-permute-start.1
  402.8 0.0 collective-permute-start.2
  402.8 7.3 %collective-permute-done = bf16[1,128,4,96,4]{1,4,0,3,2:T(4,128)(2,1)} collective-permute-done((bf16[1,128,4,96,4]{1,4,0,3,2:T(4,128)(2,1)S(1)}, bf16[1,128,4,96,4]{1,4,0,3,2:T(4,128)(2,1)}, u32[]{:S(2)}, u32[]{:S(2)}) %collective-permute-start) | collective-permute-done | bytes 393248 | tf_op jit(solution)/shard_map/ppermute | solution.py:32
  410.1 1.3 constant_dynamic-update-slice_fusion.2
  411.4 8.5 %collective-permute-done.1 = bf16[1,128,4,96,4]{1,4,0,3,2:T(4,128)(2,1)S(1)} collective-permute-done((bf16[1,128,4,96,4]{1,4,0,3,2:T(4,128)(2,1)S(1)}, bf16[1,128,4,96,4]{1,4,0,3,2:T(4,128)(2,1)S(1)}, u32[]{:S(2)}, u32[]{:S(2)}) %collective-permute-start.1) | collective-permute-done | bytes 393248 | tf_op jit(solution)/shard_map/ppermute | solution.py:32
  419.9 0.3 constant_dynamic-update-slice_fusion.1
  420.2 0.4 collective-permute-done.2
  420.6 0.3 constant_dynamic-update-slice_fusion
  420.9 2.5 copy.38
  (1 shorter events, 0.0 us)
Async XLA Ops:
  4.5 23.1 %all-to-all-start.1 = ((bf16[128,4,96,16]{0,2,1,3:T(8,128)(2,1)}), bf16[128,4,96,16]{0,2,1,3:T(8,128)(2,1)S(1)}, u32[]{:S(2)}, u32[]{:S(2)}) async-start(bf16[128,4,96,16]{0,2,1,3:T(8,128)(2,1)} %copy.26), calls=%async_computation.1 | async-start | bytes 3145728 | tf_op jit(solution)/shard_map/all_to_all | solution.py:87
  27.6 23.8 %all-to-all-start = ((bf16[128,4,96,16]{0,2,1,3:T(8,128)(2,1)}), bf16[128,4,96,16]{0,2,1,3:T(8,128)(2,1)S(1)}, u32[]{:S(2)}, u32[]{:S(2)}) async-start(bf16[128,4,96,16]{0,2,1,3:T(8,128)(2,1)} %copy.22), calls=%async_computation | async-start | bytes 3145728 | tf_op jit(solution)/shard_map/all_to_all | solution.py:81
  52.7 2.0 copy-start.1
  54.7 9.7 %copy-start.2 = (bf16[512,4,96,4]{0,2,3,1:T(8,128)(2,1)S(1)}, bf16[512,4,96,4]{0,2,3,1:T(8,128)(2,1)}, u32[]{:S(2)}) copy-start(bf16[512,4,96,4]{0,2,3,1:T(8,128)(2,1)} %all_to_all.55) | copy-start | bytes 4718596
  249.3 12.7 %copy-start = (bf16[4,8,768,96]{2,3,1,0:T(8,128)(2,1)S(1)}, bf16[4,8,768,96]{2,3,1,0:T(8,128)(2,1)}, u32[]{:S(2)}) copy-start(bf16[4,8,768,96]{2,3,1,0:T(8,128)(2,1)} %all_to_all.63) | copy-start | bytes 14155780
  303.8 73.1 %all-to-all-start.3 = ((bf16[4,4,768,96]{3,0,1,2:T(4,128)(2,1)}), bf16[4,4,768,96]{3,0,1,2:T(4,128)(2,1)S(1)}, u32[]{:S(2)}, u32[]{:S(2)}) async-start(bf16[4,4,768,96]{3,0,1,2:T(4,128)(2,1)} %copy.32), calls=%async_computation.3 | async-start | bytes 6291456 | tf_op jit(solution)/shard_map/all_to_all | solution.py:104
  399.0 11.2 %collective-permute-start = (bf16[1,128,4,96,4]{1,4,0,3,2:T(4,128)(2,1)S(1)}, bf16[1,128,4,96,4]{1,4,0,3,2:T(4,128)(2,1)}, u32[]{:S(2)}, u32[]{:S(2)}) collective-permute-start(bf16[1,128,4,96,4]{1,4,0,3,2:T(4,128)(2,1)S(1)} %get-tuple-element.11), channel_id=1, source_target_pairs={{0,1},{1,2},{2,3},{3,0},{4,5},{5,6},{6,7},{7,4},{8,9},{9,10},{10,1... | collective-permute-start | bytes 1179656 | tf_op jit(solution)/shard_map/ppermute | solution.py:32
  401.8 18.1 %collective-permute-start.1 = (bf16[1,128,4,96,4]{1,4,0,3,2:T(4,128)(2,1)S(1)}, bf16[1,128,4,96,4]{1,4,0,3,2:T(4,128)(2,1)S(1)}, u32[]{:S(2)}, u32[]{:S(2)}) collective-permute-start(bf16[1,128,4,96,4]{1,4,0,3,2:T(4,128)(2,1)S(1)} %get-tuple-element.10), channel_id=1, source_target_pairs={{0,2},{1,3},{2,0},{3,1},{4,6},{5,7},{6,4},{7,5},{8,10},{9,11},{10,... | collective-permute-start | bytes 1179656 | tf_op jit(solution)/shard_map/ppermute | solution.py:32
  402.8 17.8 %collective-permute-start.2 = (bf16[1,128,4,96,4]{1,4,0,3,2:T(4,128)(2,1)S(1)}, bf16[1,128,4,96,4]{1,4,0,3,2:T(4,128)(2,1)S(1)}, u32[]{:S(2)}, u32[]{:S(2)}) collective-permute-start(bf16[1,128,4,96,4]{1,4,0,3,2:T(4,128)(2,1)S(1)} %get-tuple-element.9), channel_id=1, source_target_pairs={{0,3},{1,0},{2,1},{3,2},{4,7},{5,4},{6,5},{7,6},{8,11},{9,8},{10,9... | collective-permute-start | bytes 1179656 | tf_op jit(solution)/shard_map/ppermute | solution.py:32
